TPU v7x, 32 devices: a whole 2x2x4 slice. The times are simulated.
32 devices in a mesh: freq: 8 (over z, x), kgrp: 4 (over y, core).
Axes of the slice: x: 2, y: 2, z: 4, core: 2. Of those that a mesh axis runs over, the one named last changes fastest.
Arguments:
- hamiltonian: float32 [256, 64, 128], P(('freq', 'kgrp')), may hold values from -1 to 1, as said below
- self_energy: float32 [16, 64, 128], P('freq'), may hold values from -0.8 to 0.3, as said below
- guess_factor: float32 [16, 64, 128], P('freq'), may hold values from -0.05 to 1.25
- weights: int32 [256], replicated, may hold values from 1 to 48
- counts: int32 [16], replicated, may hold values from 1 to 3, as said below
Outputs:
- local_green: float32 [4096, 32], P(('freq', 'kgrp'))
Inputs may be any that keep to these rules, and one draw needn't show every extreme that they name: `hamiltonian`: each k-point's matrix is Hermitian: the left half symmetric, the right half antisymmetric. `self_energy`: the diagonal of the right half lies between -0.8 and -0.4. `counts`: the number of Newton-Schulz steps taken at each frequency.
All inputs are finite; a program needn't handle non-finite values.
Results may differ from a plain program's by a relative error of at most 0.0001.
Values sent between devices are 32-bit elements.
A program may use at most 64 MiB of HBM per device.

v0:
```python
import functools
import math

import jax
import jax.numpy as jnp
from jax import lax
from jax.experimental import pallas as pl
from jax.experimental.pallas import tpu as pltpu
from jax.sharding import PartitionSpec as P

chem_potential = 0.2
MESH = pl.DeviceIdType.MESH
GRANT = 32 * 1024 * 1024
VMEM = pl.BlockSpec(memory_space=pltpu.VMEM)
SMEM = pl.BlockSpec(memory_space=pltpu.SMEM)
HBM = pl.BlockSpec(memory_space=pltpu.HBM)
LAG = 2


def split(value):
    high = value.astype(jnp.bfloat16).astype(jnp.float32)
    return high, value - high


def left_operand(value, half, left):
    high, low = split(value)
    turned_high, turned_low = split(pltpu.roll(value, half, 1))
    top = jnp.where(left, high, turned_low)
    bottom = jnp.where(left, turned_high, low)
    return jnp.concatenate([top, bottom], 0).astype(jnp.bfloat16)


def right_operand(value):
    high, low = split(value)
    row = jnp.concatenate([high, low], 1).astype(jnp.bfloat16)
    return jnp.concatenate([row, row], 0)


def fold(product, orbitals, sign):
    width = 2 * orbitals
    both = product[:, :width] + product[:, width:]
    return both[:orbitals] + sign * pltpu.roll(both[orbitals:], orbitals, 1)


def masks(shape):
    orbitals = shape[0]
    row = lax.broadcasted_iota(jnp.int32, shape, 0)
    lane = lax.broadcasted_iota(jnp.int32, shape, 1)
    left = lane < orbitals
    sign = jnp.where(left, -1.0, 1.0)
    eye_real = (lane == row).astype(jnp.float32)
    eye_imag = (lane == row + orbitals).astype(jnp.float32)
    return left, sign, eye_real, eye_imag


def shifted(freq, freq_total, eye_real, eye_imag, sigma):
    matsubara = (2 * freq + 1).astype(jnp.float32) * (math.pi / (2 * freq_total))
    return (chem_potential * eye_real + matsubara * eye_imag) - sigma


def steps_kernel(counts, weights, h_ref, sigma_ref, guess_ref, x_ref, factor_ref, m_left, h_diag):
    k_local, orbitals, width = h_ref.shape
    freq_total = sigma_ref.shape[0]
    shape = (orbitals, width)
    left, sign, eye_real, eye_imag = masks(shape)
    device = lax.axis_index("freq") * lax.axis_size("kgrp") + lax.axis_index("kgrp")

    def add_weight(index, total):
        return total + weights[index]

    weight_total = lax.fori_loop(
        0, weights.shape[0], add_weight, jnp.int32(0), unroll=8
    ).astype(jnp.float32)
    for k in range(k_local):
        weight = weights[device * k_local + k].astype(jnp.float32)
        factor_ref[k : k + 1, :] = jnp.full((1, width), weight) / weight_total

    def diagonal(value):
        real = jnp.sum(value * eye_real, axis=1, keepdims=True)
        imag = jnp.sum(value * eye_imag, axis=1, keepdims=True)
        return jnp.broadcast_to(real, shape), jnp.broadcast_to(imag, shape)

    for k in range(k_local):
        h_diag[0, k], h_diag[1, k] = diagonal(h_ref[k])

    def one_frequency(freq, carry):
        base = shifted(freq, freq_total, eye_real, eye_imag, sigma_ref[freq])
        base_real, base_imag = diagonal(base)
        guess = guess_ref[freq]
        turned = sign * pltpu.roll(guess, orbitals, 1)
        for k in range(k_local):
            real = base_real - h_diag[0, k]
            imag = base_imag - h_diag[1, k]
            inverse = 1.0 / (real * real + imag * imag)
            x_ref[freq, k] = (real * inverse) * guess - (imag * inverse) * turned

        @pl.when(counts[freq] > 1)
        def _():
            for k in range(k_local):
                m_left[k] = left_operand(base - h_ref[k], orbitals, left)

            def newton_step(sweep, inner):
                products = [
                    jnp.dot(
                        m_left[k],
                        right_operand(x_ref[freq, k]),
                        preferred_element_type=jnp.float32,
                    )
                    for k in range(k_local)
                ]
                products = [
                    jnp.dot(
                        left_operand(x_ref[freq, k], orbitals, left),
                        right_operand(eye_real - fold(products[k], orbitals, sign)),
                        preferred_element_type=jnp.float32,
                    )
                    for k in range(k_local)
                ]
                for k in range(k_local):
                    x_ref[freq, k] = x_ref[freq, k] + fold(products[k], orbitals, sign)
                return inner

            lax.fori_loop(0, counts[freq] - 1, newton_step, 0)

        return carry

    lax.fori_loop(0, freq_total, one_frequency, 0)


def early_steps(counts, weights, hamiltonian, sigma, guess):
    k_local, orbitals, width = hamiltonian.shape
    freq_total = sigma.shape[0]
    return pl.pallas_call(
        steps_kernel,
        out_shape=(
            jax.ShapeDtypeStruct((freq_total, k_local, orbitals, width), jnp.float32),
            jax.ShapeDtypeStruct((k_local, width), jnp.float32),
        ),
        in_specs=[SMEM, SMEM, VMEM, VMEM, VMEM],
        out_specs=(VMEM, VMEM),
        scratch_shapes=[
            pltpu.VMEM((k_local, width, width), jnp.bfloat16),
            pltpu.VMEM((2, k_local, orbitals, width), jnp.float32),
        ],
        compiler_params=pltpu.CompilerParams(vmem_limit_bytes=GRANT),
        name="early_steps",
    )(counts, weights, hamiltonian, sigma, guess)


def last_step(freq, freq_total, factor_ref, h_ref, sigma_ref, x_ref, last_left, last_right):
    k_local, orbitals, width = h_ref.shape
    left, sign, eye_real, eye_imag = masks((orbitals, width))
    base = shifted(freq, freq_total, eye_real, eye_imag, sigma_ref[freq])
    products = [
        jnp.dot(
            left_operand(base - h_ref[k], orbitals, left),
            right_operand(x_ref[freq, k]),
            preferred_element_type=jnp.float32,
        )
        for k in range(k_local)
    ]
    total = jnp.zeros((orbitals, width), jnp.float32)
    for k in range(k_local):
        weighted = x_ref[freq, k] * factor_ref[k : k + 1, :]
        last_left[:, k * width : (k + 1) * width] = left_operand(weighted, orbitals, left)
        total = total + weighted
    for k in range(k_local):
        missing = eye_real - fold(products[k], orbitals, sign)
        last_right[k * width : (k + 1) * width, :] = right_operand(missing)
    product = jnp.dot(last_left[...], last_right[...], preferred_element_type=jnp.float32)
    return total + fold(product, orbitals, sign)


def last_scratch(k_local, width):
    return [
        pltpu.VMEM((width, k_local * width), jnp.bfloat16),
        pltpu.VMEM((k_local * width, 2 * width), jnp.bfloat16),
    ]


def sum_kernel(factor_ref, h_ref, sigma_ref, x_ref, out_ref, last_left, last_right):
    freq_total = sigma_ref.shape[0]

    def one_frequency(freq, carry):
        out_ref[freq] = last_step(
            freq, freq_total, factor_ref, h_ref, sigma_ref, x_ref, last_left, last_right
        )
        return carry

    lax.fori_loop(0, freq_total, one_frequency, 0)


def local_sum(factors, hamiltonian, sigma, current):
    k_local, orbitals, width = hamiltonian.shape
    return pl.pallas_call(
        sum_kernel,
        out_shape=jax.ShapeDtypeStruct(sigma.shape, jnp.float32),
        in_specs=[VMEM] * 4,
        out_specs=VMEM,
        scratch_shapes=last_scratch(k_local, width),
        name="local_sum",
    )(factors, hamiltonian, sigma, current)


def halves(value):
    high = value.astype(jnp.bfloat16)
    return high, (value - high.astype(jnp.float32)).astype(jnp.bfloat16)


def joined(product):
    width = product.shape[1] // 2
    return product[:, :width] + product[:, width:]


def dot(left_side, right_side):
    return jnp.dot(left_side, right_side, preferred_element_type=jnp.float32)


def grid_of(blocks):
    return jnp.concatenate([jnp.concatenate(line, 1) for line in blocks], 0)


def gather_kernel(
    h_hbm,
    sigma_hbm,
    guess_hbm,
    weights_hbm,
    counts_hbm,
    f_out,
    rows_out,
    sg_out,
    counts_out,
    own_h,
    packed,
    weights,
    right_ref,
    g_side,
    g_shift,
    shift_rows,
    h_rows,
    scales,
    local,
    mate_sem,
    pair_sem,
    pass_sem,
    col_sem,
):
    column, slots, pairs, _, orbitals, width = f_out.shape
    k_local = 2 * pairs
    shape = (orbitals, width)
    freq_devs = 2 * column
    freq_total = 2 * freq_devs
    me = lax.axis_index("freq")
    group = lax.axis_index("kgrp")
    group_devs = lax.axis_size("kgrp")
    parity = lax.rem(group, 2)
    branch = lax.rem(me, 2)
    place = me // 2
    pair = me + 1 - 2 * branch
    mate = group + 1 - 2 * parity
    others = [place + 1 - 2 * lax.rem(place, 2), lax.rem(place + 2, column), column - 1 - place]
    barrier = pltpu.get_barrier_semaphore()
    for other in others:
        pl.semaphore_signal(barrier, inc=1, device_id=(2 * other + branch, group), device_id_type=MESH)
    pl.semaphore_signal(barrier, inc=1, device_id=(pair, group), device_id_type=MESH)
    pl.semaphore_signal(barrier, inc=1, device_id=(me, mate), device_id_type=MESH)
    loads = [
        pltpu.make_async_copy(h_hbm, own_h, local.at[0]),
        pltpu.make_async_copy(sigma_hbm.at[parity], sg_out.at[place, 0], local.at[1]),
        pltpu.make_async_copy(guess_hbm.at[parity], sg_out.at[place, 1], local.at[2]),
        pltpu.make_async_copy(weights_hbm, weights, local.at[3]),
        pltpu.make_async_copy(counts_hbm, counts_out, local.at[4]),
    ]
    for load in loads:
        load.start()

    def remote(src, dst, sems, slot, freq_to, group_to):
        return pltpu.make_async_remote_copy(
            src_ref=src,
            dst_ref=dst,
            send_sem=sems.at[0, slot],
            recv_sem=sems.at[1, slot],
            device_id=(freq_to, group_to),
            device_id_type=MESH,
        )

    own = sg_out.at[place]
    columns = [
        remote(own, own, col_sem, index, 2 * others[index] + branch, group) for index in range(column - 1)
    ]
    across = [remote(packed.at[0, c], packed.at[2, c], pair_sem, c, pair, group) for c in range(pairs)]
    passes = [remote(packed.at[2, c], packed.at[3, c], pass_sem, c, me, mate) for c in range(pairs)]
    beside = remote(packed.at[0], packed.at[1], mate_sem, 0, me, mate)

    row = lax.broadcasted_iota(jnp.int32, shape, 0)
    lane = lax.broadcasted_iota(jnp.int32, shape, 1)
    left = lane < orbitals
    within = jnp.where(left, lane, lane - orbitals)
    upper = within >= row
    above = within > row
    eye_both = (within == row).astype(jnp.float32)

    def turn(value):
        return pltpu.roll(value, orbitals, 1)

    def planes(slot, c, real, imag):
        diagonal = jnp.sum(eye_both * real, axis=0, keepdims=True)
        h_rows[slot, c : c + 1, :] = diagonal
        h_rows[slot, pairs + c : pairs + c + 1, :] = diagonal
        for part, (r, i) in enumerate(zip(halves(real), halves(imag))):
            right_ref[slot, c, part] = grid_of([[r, i], [-i, r]])

    loads[0].wait()
    for c in range(pairs):
        one, two = own_h[2 * c], own_h[2 * c + 1]
        real = jnp.where(left, one, turn(two))
        imag = jnp.where(left, turn(one), two)
        packed[0, c] = jnp.where(upper, real, imag)
    loads[1].wait()
    loads[2].wait()
    pl.semaphore_wait(barrier, column + 1)
    for copy in across + columns + [beside]:
        copy.start()
    loads[3].wait()
    loads[4].wait()

    def times(guess_side, right_high, right_low):
        return dot(guess_side, jnp.concatenate([right_high, right_high, right_low], 0))

    def prepare(index):
        frequency = 2 * (2 * index + branch) + parity
        matsubara = (2 * frequency + 1).astype(jnp.float32) * (math.pi / (2 * freq_total))
        sigma = sg_out[index, 0]
        swapped = turn(sigma)
        real = chem_potential * eye_both - jnp.where(left, sigma, swapped)
        imag = matsubara * eye_both - jnp.where(left, swapped, sigma)
        high, low = halves(sg_out[index, 1])
        guess_side = jnp.concatenate([high, low, high], 1)
        g_side[index] = guess_side
        shift_rows[index, 0] = jnp.broadcast_to(jnp.sum(eye_both * real, axis=0, keepdims=True), tile)
        shift_rows[index, 1] = jnp.broadcast_to(jnp.sum(eye_both * imag, axis=0, keepdims=True), tile)
        (real_high, real_low), (imag_high, imag_low) = halves(real), halves(imag)
        product = times(
            guess_side,
            grid_of([[real_high, imag_high], [-imag_high, real_high]]),
            grid_of([[real_low, imag_low], [-imag_low, real_low]]),
        )
        g_shift[index] = product

    def unpack(slot):
        for c in range(pairs):
            value = packed[slot, c]
            flipped = jnp.transpose(value)
            other = jnp.concatenate([flipped[:orbitals], flipped[orbitals:]], 1)
            real = jnp.where(upper, value, other)
            imag = jnp.where(above, -other, jnp.where(upper, 0.0, value))
            planes(slot, c, real, imag)

    tile = (2 * pairs, width)
    tile_row = lax.broadcasted_iota(jnp.int32, tile, 0)
    tile_left = lax.broadcasted_iota(jnp.int32, tile, 1) < orbitals
    tile_real = tile_row < pairs
    tile_k = 2 * jnp.where(tile_real, tile_row, tile_row - pairs) + jnp.where(tile_left, 0, 1)

    def slot_weights(slot):
        owner_freq = me + (slot // 2) * (1 - 2 * branch)
        owner_group = group + (slot % 2) * (1 - 2 * parity)
        k_first = (owner_freq * group_devs + owner_group) * k_local
        first_row, first_column = lax.div(k_first, width), lax.rem(k_first, width)
        weight = jnp.zeros(tile, jnp.float32)
        for j in range(k_local):
            value = weights[first_row, first_column + j].astype(jnp.float32)
            weight = jnp.where(tile_k == j, value, weight)
        return weight

    def apply(at_slots, indices):
        for slot in at_slots:
            weight = slot_weights(slot)
            for index in indices:
                real = shift_rows[index, 0] - h_rows[slot]
                imag = shift_rows[index, 1]
                inverse = 1.0 / (real * real + imag * imag)
                scale = jnp.where(tile_real, real * inverse, -imag * inverse)
                scales[index, slot] = scale
                rows_out[index, slot] = weight * scale
        side = jnp.concatenate([g_side[index] for index in indices], 0)
        for slot in at_slots:
            for c in range(pairs):
                product = times(side, right_ref[slot, c, 0], right_ref[slot, c, 1])
                for at, index in enumerate(indices):
                    q = g_shift[index] - product[at * orbitals : (at + 1) * orbitals]
                    d_real = scales[index, slot, c : c + 1, :]
                    d_imag = scales[index, slot, pairs + c : pairs + c + 1, :]
                    real, imag = q[:, :width], q[:, width:]
                    f_out[index, slot, c, 0] = eye_both - real * d_real + imag * d_imag
                    f_out[index, slot, c, 1] = -real * d_imag - imag * d_real

    prepare(place)
    unpack(0)
    apply([0], [place])
    beside.wait_recv()
    unpack(1)
    apply([1], [place])
    for index in range(column - 2):
        columns[index].wait_recv()
        prepare(others[index])
        apply([0, 1], [others[index]])
        for c in range(2 * index, 2 * index + 2):
            across[c].wait_recv()
            passes[c].start()
    early = [place] + others[:-1]
    unpack(2)
    apply([2], early)
    for copy in passes:
        copy.wait_recv()
    unpack(3)
    apply([3], early)
    columns[-1].wait_recv()
    prepare(others[-1])
    apply(range(slots), [others[-1]])
    for copy in columns + across + passes + [beside]:
        copy.wait_send()


def gather(hamiltonian, self_energy, guess_factor, weights, counts, column):
    k_local, orbitals, width = hamiltonian.shape
    pairs = k_local // 2
    return pl.pallas_call(
        gather_kernel,
        out_shape=(
            jax.ShapeDtypeStruct((column, 4, pairs, 2, orbitals, width), jnp.float32),
            jax.ShapeDtypeStruct((column, 4, k_local, width), jnp.float32),
            jax.ShapeDtypeStruct((column, 2, orbitals, width), jnp.float32),
            jax.ShapeDtypeStruct(counts.shape, jnp.int32),
        ),
        in_specs=[HBM] * 5,
        out_specs=(VMEM,) * 4,
        scratch_shapes=[
            pltpu.VMEM((k_local, orbitals, width), jnp.float32),
            pltpu.VMEM((4, pairs, orbitals, width), jnp.float32),
            pltpu.SMEM(weights.shape, jnp.int32),
            pltpu.VMEM((4, pairs, 2, width, 2 * width), jnp.bfloat16),
            pltpu.VMEM((column, orbitals, 3 * width), jnp.bfloat16),
            pltpu.VMEM((column, orbitals, 2 * width), jnp.float32),
            pltpu.VMEM((column, 2, k_local, width), jnp.float32),
            pltpu.VMEM((4, k_local, width), jnp.float32),
            pltpu.VMEM((column, 4, k_local, width), jnp.float32),
            pltpu.SemaphoreType.DMA((5,)),
            pltpu.SemaphoreType.DMA((2, 1)),
            pltpu.SemaphoreType.DMA((2, pairs)),
            pltpu.SemaphoreType.DMA((2, pairs)),
            pltpu.SemaphoreType.DMA((2, column)),
        ],
        compiler_params=pltpu.CompilerParams(collective_id=0, has_side_effects=True, vmem_limit_bytes=GRANT),
        name="gather",
    )(hamiltonian, self_energy, guess_factor, weights, counts)


def newton_kernel(f_ref, rows, counts_ref, left_ref, right_ref, work, counts):
    column, slots, pairs, _, orbitals, width = f_ref.shape
    total_pairs = slots * pairs
    shape = (orbitals, width)
    parity = lax.rem(lax.axis_index("kgrp"), 2)
    branch = lax.rem(lax.axis_index("freq"), 2)
    steps = counts_ref[...]
    step_lane = lax.broadcasted_iota(jnp.int32, steps.shape, 1)
    for index in range(column):
        counts[index] = jnp.sum(jnp.where(step_lane == 2 * (2 * index + branch) + parity, steps, 0))
    row = lax.broadcasted_iota(jnp.int32, shape, 0)
    lane = lax.broadcasted_iota(jnp.int32, shape, 1)
    left = lane < orbitals
    eye_both = (lax.rem(lane, orbitals) == row).astype(jnp.float32)
    eye_half = eye_both.astype(jnp.bfloat16)
    left_half = left.astype(jnp.float32).astype(jnp.bfloat16)
    right_half = (1.0 - left.astype(jnp.float32)).astype(jnp.bfloat16)

    def turn(value):
        return pltpu.roll(value, orbitals, 1)

    def spread(real, imag):
        real_left, real_right = real * left_half, real * right_half
        imag_left, imag_right = imag * left_half, imag * right_half
        return grid_of(
            [
                [real_left, imag_left],
                [real_right, imag_right],
                [-imag_left, real_left],
                [-imag_right, real_right],
            ]
        )

    def parts(real, imag):
        (real_high, real_low), (imag_high, imag_low) = halves(real), halves(imag)
        return (real_high, imag_high), (real_low, imag_low)

    def multiply(highs, lows, right_high, right_low):
        count = len(highs) * orbitals
        high = jnp.concatenate(highs, 0)
        both = dot(jnp.concatenate([high] + lows, 0), spread(*right_high))
        return both[:count] + both[count:] + dot(high, spread(*right_low))

    def beside(pair):
        return jnp.concatenate(pair, 1)

    def one_frequency(index, carry):
        count = counts[index]

        def load_f(p):
            return f_ref[index, p // pairs, p % pairs, 0], f_ref[index, p // pairs, p % pairs, 1]

        lines = []
        for slot in range(slots):
            line = rows[index, slot]
            lines += [line, turn(line)]
        lines.append(jnp.zeros((width - 4 * pairs * slots, width), jnp.float32))
        flat = jnp.transpose(jnp.concatenate(lines, 0))[:orbitals]

        def column_of(at):
            return jnp.take_along_axis(flat, jnp.where(left, at, at + 2 * pairs), axis=1)

        def scaled(p, real, imag):
            first = (p // pairs) * 4 * pairs + p % pairs
            d_real, d_imag = column_of(first), column_of(first + pairs)
            return real * d_real - imag * d_imag, real * d_imag + imag * d_real

        def squares(p):
            real, imag = load_f(p)
            high, low = parts(real, imag)
            product = multiply([beside(high)], [beside(low)], high, low)
            work[p, 0] = product[:, :width]
            work[p, 1] = product[:, width:]

        def cubes(p):
            real, imag = load_f(p)
            square_real, square_imag = work[p, 0], work[p, 1]
            high, low = parts(real, imag)
            square_high, square_low = parts(square_real, square_imag)
            product = multiply(
                [beside(high), beside(square_high)],
                [beside(low), beside(square_low)],
                square_high,
                square_low,
            )
            work[p, 2] = eye_both + real + square_real + product[:orbitals, :width]
            work[p, 3] = imag + square_imag + product[:orbitals, width:]
            work[p, 4] = product[orbitals:, :width]
            work[p, 5] = product[orbitals:, width:]

        def store_left(p, high, low):
            left_ref[index, :orbitals, 2 * p * width : 2 * (p + 1) * width] = beside(high)
            left_ref[index, orbitals:, 2 * p * width : 2 * (p + 1) * width] = beside(low)

        def store_right(p, real, imag):
            lines = []
            for r, i in parts(eye_both + real, imag):
                r_turned, i_turned = turn(r), turn(i)
                lines.append(
                    [
                        r * left_half + i_turned * right_half,
                        r_turned * left_half + i * right_half,
                        r_turned * right_half - i * left_half,
                        r * right_half - i_turned * left_half,
                    ]
                )
            right_ref[index, 2 * p * width : 2 * (p + 1) * width, :] = grid_of(list(zip(*lines)))

        def finish(p, outer, inner):
            store_left(p, *parts(*scaled(p, *outer)))
            store_right(p, *inner)

        @pl.when(count == 1)
        def _():
            for p in range(total_pairs):
                slot, c = p // pairs, p % pairs
                store_left(
                    p,
                    *[
                        [eye_half * line[at : at + 1, :] for at in (c, pairs + c)]
                        for line in halves(rows[index, slot])
                    ],
                )
                store_right(p, *load_f(p))

        @pl.when(count == 2)
        def _():
            for step in range(total_pairs + LAG):
                if step < total_pairs:
                    squares(step)
                if step >= LAG:
                    p = step - LAG
                    real, imag = load_f(p)
                    finish(p, (eye_both + real, imag), (work[p, 0], work[p, 1]))

        @pl.when(count > 2)
        def _():
            for step in range(total_pairs + 2 * LAG):
                if step < total_pairs:
                    squares(step)
                if LAG <= step < total_pairs + LAG:
                    cubes(step - LAG)
                if step >= 2 * LAG:
                    p = step - 2 * LAG
                    finish(p, (work[p, 2], work[p, 3]), (work[p, 4], work[p, 5]))

        return carry

    lax.fori_loop(0, column, one_frequency, 0)


def newton(f_values, rows, counts):
    column, slots, pairs, _, orbitals, width = f_values.shape
    depth = 2 * slots * pairs * width
    return pl.pallas_call(
        newton_kernel,
        out_shape=(
            jax.ShapeDtypeStruct((column, 2 * orbitals, depth), jnp.bfloat16),
            jax.ShapeDtypeStruct((column, depth, 2 * width), jnp.bfloat16),
        ),
        in_specs=[VMEM] * 3,
        out_specs=(VMEM, VMEM),
        scratch_shapes=[
            pltpu.VMEM((slots * pairs, 6, orbitals, width), jnp.float32),
            pltpu.SMEM((column,), jnp.int32),
        ],
        compiler_params=pltpu.CompilerParams(vmem_limit_bytes=GRANT),
        name="newton",
    )(f_values, rows, counts)


def scatter_kernel(left_ref, right_ref, sg_ref, weights_hbm, out_ref, weights, part, landed, load_sem, send, recv):
    freq_devs = lax.axis_size("freq")
    group_devs = lax.axis_size("kgrp")
    column, _, orbitals, width = sg_ref.shape
    tile = landed.shape[2]
    me = lax.axis_index("freq")
    group = lax.axis_index("kgrp")
    others = [(a, b) for a in range(freq_devs) for b in range(group_devs) if a + b > 0]
    barrier = pltpu.get_barrier_semaphore()

    def place(step):
        return lax.rem(me + step[0], freq_devs), lax.rem(group + step[1], group_devs)

    for step in others:
        pl.semaphore_signal(barrier, inc=1, device_id=place(step), device_id_type=MESH)
    load = pltpu.make_async_copy(weights_hbm, weights, load_sem.at[0])
    load.start()

    def spread(index):
        freq_to, group_to = place(others[index])
        return pltpu.make_async_remote_copy(
            src_ref=part.at[pl.ds((freq_to * group_devs + group_to) * tile, tile)],
            dst_ref=landed.at[me, group],
            send_sem=send.at[index],
            recv_sem=recv.at[index],
            device_id=(freq_to, group_to),
            device_id_type=MESH,
        )

    wide_left = lax.broadcasted_iota(jnp.int32, (orbitals, width), 1) < orbitals
    depth = left_ref.shape[2]
    step = 2 * width
    products = []
    for first in range(0, column, 2):
        sums = [None, None]
        for at in range(0, depth, step):
            for offset in range(2):
                index = first + offset
                term = dot(left_ref[index, :, at : at + step], right_ref[index, at : at + step, :])
                sums[offset] = term if at == 0 else sums[offset] + term
        products += sums
    for index in range(column):
        guess = sg_ref[index, 1]
        turned = pltpu.roll(guess, orbitals, 1)
        top = jnp.concatenate(halves(guess), 1)
        bottom = jnp.concatenate(halves(jnp.where(wide_left, -turned, turned)), 1)
        product = products[index]
        total = joined(product[:orbitals]) + product[orbitals:, :width]
        left_side = jnp.concatenate(halves(total), 1)
        green = joined(dot(left_side, jnp.concatenate([top, bottom, top, bottom], 0)))
        part[pl.ds(index, orbitals, stride=column), :] = green
    pl.semaphore_wait(barrier, len(others))
    for index in range(len(others)):
        spread(index).start()
    landed[me, group] = part[pl.ds((me * group_devs + group) * tile, tile), :]
    load.wait()
    total = jnp.sum(weights[...].astype(jnp.float32), axis=0, keepdims=True)
    scale = 1.0 / jnp.broadcast_to(jnp.sum(total, axis=1, keepdims=True), (tile, width))
    for index in range(len(others)):
        spread(index).wait_recv()
    left = lax.broadcasted_iota(jnp.int32, (tile, width), 1) < orbitals
    freq_total = 4 * column
    for branch in range(2):
        for parity in range(2):
            total = None
            for place_at in range(column):
                for high in range(group_devs // 2):
                    term = landed[2 * place_at + branch, 2 * high + parity]
                    total = term if total is None else total + term
            total = total * scale
            swapped = pltpu.roll(total, tile // 2, 0)
            turned = pltpu.roll(total, orbitals, 1)
            turned_swapped = pltpu.roll(turned, tile // 2, 0)
            real = jnp.where(left, total, turned_swapped)
            imag = jnp.where(left, turned, swapped)
            first = 2 * branch + parity
            out_ref[pl.ds(first, column, stride=4), :] = real[:column]
            out_ref[pl.ds(freq_total + first, column, stride=4), :] = imag[:column]
    for index in range(len(others)):
        spread(index).wait_send()


def scatter(left, right, sigma_guess, weights, freq_devs, group_devs):
    column, _, orbitals, width = sigma_guess.shape
    tile = column * orbitals // (freq_devs * group_devs)
    peers = freq_devs * group_devs - 1
    return pl.pallas_call(
        scatter_kernel,
        out_shape=jax.ShapeDtypeStruct((8 * column, width), jnp.float32),
        in_specs=[VMEM, VMEM, VMEM, HBM],
        out_specs=VMEM,
        scratch_shapes=[
            pltpu.VMEM(weights.shape, jnp.int32),
            pltpu.VMEM((column * orbitals, width), jnp.float32),
            pltpu.VMEM((freq_devs, group_devs, tile, width), jnp.float32),
            pltpu.SemaphoreType.DMA((1,)),
            pltpu.SemaphoreType.DMA((peers,)),
            pltpu.SemaphoreType.DMA((peers,)),
        ],
        compiler_params=pltpu.CompilerParams(collective_id=1, has_side_effects=True, vmem_limit_bytes=GRANT),
        name="scatter",
    )(left, right, sigma_guess, weights)


def per_device(hamiltonian, self_energy, guess_factor, weights, counts):
    k_local, orbitals, width = hamiltonian.shape
    per_freq = self_energy.shape[0]
    freq_devs = lax.axis_size("freq")
    group_devs = lax.axis_size("kgrp")
    freq_total = per_freq * freq_devs
    pair_block = orbitals * orbitals // (freq_devs * group_devs)
    column = freq_devs // 2
    direct = (
        width == 128
        and per_freq == 2
        and freq_devs % 2 == 0
        and group_devs % 2 == 0
        and pair_block == width
        and column == 4
        and k_local == 8
        and weights.shape[0] % width == 0
    )
    if direct:
        table = weights.reshape(-1, width)
        inputs = [
            pltpu.with_memory_space_constraint(value, pltpu.HBM)
            for value in (hamiltonian, self_energy, guess_factor, table, counts.reshape(1, -1))
        ]
        values, rows, sigma_guess, steps = gather(*inputs, column)
        left, right = newton(values, rows, steps)
        return scatter(left, right, sigma_guess, inputs[3], freq_devs, group_devs).T
    sigma = lax.all_gather(self_energy, "freq", axis=0, tiled=True)
    guess = lax.all_gather(guess_factor, "freq", axis=0, tiled=True)
    current, factors = early_steps(counts, weights, hamiltonian, sigma, guess)
    terms = local_sum(factors, hamiltonian, sigma, current)
    terms = terms.reshape(freq_total, orbitals, 2, orbitals).transpose(1, 3, 2, 0)
    terms = terms.reshape(orbitals * orbitals, 2 * freq_total)
    result = lax.psum_scatter(terms, ("freq", "kgrp"), scatter_dimension=0, tiled=True)
    return result.reshape(pair_block, 2 * freq_total)


def solution(mesh):
    return jax.shard_map(
        per_device,
        mesh=mesh,
        in_specs=(
            P(("freq", "kgrp"), None, None),
            P("freq", None, None),
            P("freq", None, None),
            P(),
            P(),
        ),
        out_specs=P(("freq", "kgrp"), None),
        check_vma=False,
    )
```

profile of v0, /device:TPU:0, one launch (start us, length us, event | category | flops | bytes accessed | tf_op | source)
XLA Modules:
  0.0 27.2 jit_solution(15165142350661071376)
XLA Ops:
  0.0 12.2 %gather.1 = (f32[4,4,4,2,64,128]{5,4,3,2,1,0:T(8,128)S(1)}, f32[4,4,8,128]{3,2,1,0:T(8,128)S(1)}, f32[4,2,64,128]{3,2,1,0:T(8,128)S(1)}, s32[1,16]{1,0:T(1,128)S(1)}) custom-call(f32[8,64,128]{2,1,0:T(8,128)} %h_hbm.1, f32[2,64,128]{2,1,0:T(8,128)} %sigma_hbm.1, f32[2,64,128]{2,1,0:T(8,128)} %guess_hbm.1, s32[2,128]{1,0:T(2,128)} %bitcast.4, s32[1,16]{1,0:T(1,128)} %bitcast.6), custom_call_target="tpu_custom_call" | custom-call | tf_op jit(solution)/shard_map/gather/pallas_call | solution.py:428
  12.2 5.8 %newton.1 = (bf16[4,128,4096]{2,1,0:T(8,128)(2,1)S(1)}, bf16[4,4096,256]{2,1,0:T(8,128)(2,1)S(1)}) custom-call(f32[4,4,4,2,64,128]{5,4,3,2,1,0:T(8,128)S(1)} %get-tuple-element.11.f_ref, f32[4,4,8,128]{3,2,1,0:T(8,128)S(1)} %get-tuple-element.12.rows, s32[1,16]{1,0:T(1,128)S(1)} %get-tuple-element.13.counts_ref), custom_call_target="tpu_custom_call" | custom-call | tf_op jit(solution)/shard_map/newton/pallas_call | solution.py:613
  18.0 8.6 %scatter.1 = f32[32,128]{1,0:T(8,128)S(1)} custom-call(bf16[4,128,4096]{2,1,0:T(8,128)(2,1)S(1)} %get-tuple-element.14.left_ref, bf16[4,4096,256]{2,1,0:T(8,128)(2,1)S(1)} %get-tuple-element.15.right_ref, f32[4,2,64,128]{3,2,1,0:T(8,128)S(1)} %get-tuple-element.16.sg_ref, s32[2,128]{1,0:T(2,128)} %bitcast.5), custom_call_target="tpu_custom_call" | custom-call | tf_op jit(solution)/shard_map/scatter/pallas_call | solution.py:716
  26.6 0.6 %copy.7 = f32[128,32]{0,1:T(8,128)} copy(f32[128,32]{0,1:T(8,128)S(1)} %bitcast.3) | data formatting | bytes 32768
where the time goes:
time: 27.2 us
  Pallas kernels  26.6 us (98%)
  local copies, waits for them, and re-layouts  0.61 us (2%)
    pallas_call x1, Pallas kernels, gather(): pl.pallas_call(gather_kernel, out_shape=(jax.ShapeDtypeStruct((column, 4,...  12.2 us
    pallas_call x1, Pallas kernels, scatter(): pl.pallas_call(scatter_kernel, out_shape=jax.ShapeDtypeStruct((8 * column...  8.62 us
    pallas_call x1, Pallas kernels, newton(): pl.pallas_call(newton_kernel, out_shape=(jax.ShapeDtypeStruct((column, 2...  5.79 us
    unnamed x1, local copies, waits for them, and re-layouts  0.61 us

commit v1 on v0

--- a/solution.py
+++ b/solution.py
@@ -14,7 +14,8 @@
 VMEM = pl.BlockSpec(memory_space=pltpu.VMEM)
 SMEM = pl.BlockSpec(memory_space=pltpu.SMEM)
 HBM = pl.BlockSpec(memory_space=pltpu.HBM)
-LAG = 2
+LAG = 4
+TAIL = 4
 
 
 def split(value):
@@ -397,27 +398,24 @@
 
     prepare(place)
     unpack(0)
-    apply([0], [place])
     beside.wait_recv()
     unpack(1)
-    apply([1], [place])
-    for index in range(column - 2):
-        columns[index].wait_recv()
-        prepare(others[index])
-        apply([0, 1], [others[index]])
-        for c in range(2 * index, 2 * index + 2):
-            across[c].wait_recv()
-            passes[c].start()
-    early = [place] + others[:-1]
+    columns[0].wait_recv()
+    prepare(others[0])
+    apply([0, 1], [place, others[0]])
+    for c in range(pairs):
+        across[c].wait_recv()
+        passes[c].start()
     unpack(2)
-    apply([2], early)
+    apply([2], [place, others[0]])
     for copy in passes:
         copy.wait_recv()
     unpack(3)
-    apply([3], early)
-    columns[-1].wait_recv()
-    prepare(others[-1])
-    apply(range(slots), [others[-1]])
+    apply([3], [place, others[0]])
+    for index in range(1, column - 1):
+        columns[index].wait_recv()
+        prepare(others[index])
+    apply(range(slots), others[1:])
     for copy in columns + across + passes + [beside]:
         copy.wait_send()
 
@@ -456,30 +454,84 @@
     )(hamiltonian, self_energy, guess_factor, weights, counts)
 
 
-def newton_kernel(f_ref, rows, counts_ref, left_ref, right_ref, work, counts):
+class Tools:
+    def __init__(self, orbitals, width):
+        self.orbitals, self.width = orbitals, width
+        shape = (orbitals, width)
+        row = lax.broadcasted_iota(jnp.int32, shape, 0)
+        lane = lax.broadcasted_iota(jnp.int32, shape, 1)
+        self.left = lane < orbitals
+        self.eye_both = (lax.rem(lane, orbitals) == row).astype(jnp.float32)
+        self.eye_half = self.eye_both.astype(jnp.bfloat16)
+        self.left_half = self.left.astype(jnp.float32).astype(jnp.bfloat16)
+        self.right_half = (1.0 - self.left.astype(jnp.float32)).astype(jnp.bfloat16)
+        self.left_mask = self.left_half > self.right_half
+
+    def turn(self, value):
+        return pltpu.roll(value, self.orbitals, 1)
+
+    def columns(self, rows, index):
+        slots, lines_each = rows.shape[1], rows.shape[2]
+        lines = []
+        for slot in range(slots):
+            line = rows[index, slot]
+            lines += [line, self.turn(line)]
+        lines.append(jnp.zeros((self.width - 2 * lines_each * slots, self.width), jnp.float32))
+        return jnp.transpose(jnp.concatenate(lines, 0))[: self.orbitals]
+
+    def scaled(self, flat, pairs, p, real, imag):
+        def column_of(at):
+            return jnp.take_along_axis(flat, jnp.where(self.left, at, at + 2 * pairs), axis=1)
+
+        first = (p // pairs) * 4 * pairs + p % pairs
+        d_real, d_imag = column_of(first), column_of(first + pairs)
+        return real * d_real - imag * d_imag, real * d_imag + imag * d_real
+
+    def store_left(self, ref, index, at, high, low):
+        span = slice(2 * at * self.width, 2 * (at + 1) * self.width)
+        ref[index, : self.orbitals, span] = beside(high)
+        ref[index, self.orbitals :, span] = beside(low)
+
+    def store_right(self, ref, index, at, real, imag):
+        lines = []
+        for r, i in parts(self.eye_both + real, imag):
+            r_turned, i_turned = self.turn(r), self.turn(i)
+            lines.append(
+                [
+                    jnp.where(self.left_mask, r, i_turned),
+                    jnp.where(self.left_mask, r_turned, i),
+                    jnp.where(self.left_mask, -i, r_turned),
+                    jnp.where(self.left_mask, -i_turned, r),
+                ]
+            )
+        ref[index, 2 * at * self.width : 2 * (at + 1) * self.width, :] = grid_of(list(zip(*lines)))
+
+
+def parts(real, imag):
+    (real_high, real_low), (imag_high, imag_low) = halves(real), halves(imag)
+    return (real_high, imag_high), (real_low, imag_low)
+
+
+def beside(pair):
+    return jnp.concatenate(pair, 1)
+
+
+def newton_kernel(f_ref, rows, counts_ref, left_ref, right_ref, tail_ref, work, sides, counts):
     column, slots, pairs, _, orbitals, width = f_ref.shape
     total_pairs = slots * pairs
-    shape = (orbitals, width)
+    kept = total_pairs - tail_ref.shape[1]
     parity = lax.rem(lax.axis_index("kgrp"), 2)
     branch = lax.rem(lax.axis_index("freq"), 2)
     steps = counts_ref[...]
     step_lane = lax.broadcasted_iota(jnp.int32, steps.shape, 1)
     for index in range(column):
         counts[index] = jnp.sum(jnp.where(step_lane == 2 * (2 * index + branch) + parity, steps, 0))
-    row = lax.broadcasted_iota(jnp.int32, shape, 0)
-    lane = lax.broadcasted_iota(jnp.int32, shape, 1)
-    left = lane < orbitals
-    eye_both = (lax.rem(lane, orbitals) == row).astype(jnp.float32)
-    eye_half = eye_both.astype(jnp.bfloat16)
-    left_half = left.astype(jnp.float32).astype(jnp.bfloat16)
-    right_half = (1.0 - left.astype(jnp.float32)).astype(jnp.bfloat16)
-
-    def turn(value):
-        return pltpu.roll(value, orbitals, 1)
+    tools = Tools(orbitals, width)
+    eye_both = tools.eye_both
 
     def spread(real, imag):
-        real_left, real_right = real * left_half, real * right_half
-        imag_left, imag_right = imag * left_half, imag * right_half
+        real_left, real_right = real * tools.left_half, real * tools.right_half
+        imag_left, imag_right = imag * tools.left_half, imag * tools.right_half
         return grid_of(
             [
                 [real_left, imag_left],
@@ -489,118 +541,98 @@
             ]
         )
 
-    def parts(real, imag):
-        (real_high, real_low), (imag_high, imag_low) = halves(real), halves(imag)
-        return (real_high, imag_high), (real_low, imag_low)
-
     def multiply(highs, lows, right_high, right_low):
         count = len(highs) * orbitals
         high = jnp.concatenate(highs, 0)
         both = dot(jnp.concatenate([high] + lows, 0), spread(*right_high))
         return both[:count] + both[count:] + dot(high, spread(*right_low))
 
-    def beside(pair):
-        return jnp.concatenate(pair, 1)
-
     def one_frequency(index, carry):
         count = counts[index]
 
         def load_f(p):
             return f_ref[index, p // pairs, p % pairs, 0], f_ref[index, p // pairs, p % pairs, 1]
-
-        lines = []
-        for slot in range(slots):
-            line = rows[index, slot]
-            lines += [line, turn(line)]
-        lines.append(jnp.zeros((width - 4 * pairs * slots, width), jnp.float32))
-        flat = jnp.transpose(jnp.concatenate(lines, 0))[:orbitals]
-
-        def column_of(at):
-            return jnp.take_along_axis(flat, jnp.where(left, at, at + 2 * pairs), axis=1)
-
-        def scaled(p, real, imag):
-            first = (p // pairs) * 4 * pairs + p % pairs
-            d_real, d_imag = column_of(first), column_of(first + pairs)
-            return real * d_real - imag * d_imag, real * d_imag + imag * d_real
 
         def squares(p):
             real, imag = load_f(p)
             high, low = parts(real, imag)
+            sides[p, 0], sides[p, 1] = beside(high), beside(low)
             product = multiply([beside(high)], [beside(low)], high, low)
             work[p, 0] = product[:, :width]
             work[p, 1] = product[:, width:]
 
+        def keep(p, values):
+            for at, value in enumerate(values):
+                if p >= kept:
+                    tail_ref[index, p - kept, at] = value
+                else:
+                    work[p, 2 + at] = value
+
         def cubes(p):
             real, imag = load_f(p)
             square_real, square_imag = work[p, 0], work[p, 1]
-            high, low = parts(real, imag)
             square_high, square_low = parts(square_real, square_imag)
             product = multiply(
-                [beside(high), beside(square_high)],
-                [beside(low), beside(square_low)],
+                [sides[p, 0], beside(square_high)],
+                [sides[p, 1], beside(square_low)],
                 square_high,
                 square_low,
             )
-            work[p, 2] = eye_both + real + square_real + product[:orbitals, :width]
-            work[p, 3] = imag + square_imag + product[:orbitals, width:]
-            work[p, 4] = product[orbitals:, :width]
-            work[p, 5] = product[orbitals:, width:]
-
-        def store_left(p, high, low):
-            left_ref[index, :orbitals, 2 * p * width : 2 * (p + 1) * width] = beside(high)
-            left_ref[index, orbitals:, 2 * p * width : 2 * (p + 1) * width] = beside(low)
-
-        def store_right(p, real, imag):
-            lines = []
-            for r, i in parts(eye_both + real, imag):
-                r_turned, i_turned = turn(r), turn(i)
-                lines.append(
-                    [
-                        r * left_half + i_turned * right_half,
-                        r_turned * left_half + i * right_half,
-                        r_turned * right_half - i * left_half,
-                        r * right_half - i_turned * left_half,
-                    ]
-                )
-            right_ref[index, 2 * p * width : 2 * (p + 1) * width, :] = grid_of(list(zip(*lines)))
-
-        def finish(p, outer, inner):
-            store_left(p, *parts(*scaled(p, *outer)))
-            store_right(p, *inner)
+            keep(
+                p,
+                [
+                    eye_both + real + square_real + product[:orbitals, :width],
+                    imag + square_imag + product[:orbitals, width:],
+                    product[orbitals:, :width],
+                    product[orbitals:, width:],
+                ],
+            )
+
+        def finish(flat, p, outer, inner):
+            high, low = parts(*tools.scaled(flat, pairs, p, *outer))
+            tools.store_left(left_ref, index, p, high, low)
+            tools.store_right(right_ref, index, p, *inner)
 
         @pl.when(count == 1)
         def _():
             for p in range(total_pairs):
                 slot, c = p // pairs, p % pairs
-                store_left(
-                    p,
-                    *[
-                        [eye_half * line[at : at + 1, :] for at in (c, pairs + c)]
-                        for line in halves(rows[index, slot])
-                    ],
-                )
-                store_right(p, *load_f(p))
+                real, imag = load_f(p)
+                if p >= kept:
+                    keep(p, [eye_both, jnp.zeros_like(eye_both), real, imag])
+                    continue
+                high, low = [
+                    [tools.eye_half * line[at : at + 1, :] for at in (c, pairs + c)]
+                    for line in halves(rows[index, slot])
+                ]
+                tools.store_left(left_ref, index, p, high, low)
+                tools.store_right(right_ref, index, p, real, imag)
 
         @pl.when(count == 2)
         def _():
+            flat = tools.columns(rows, index)
             for step in range(total_pairs + LAG):
                 if step < total_pairs:
                     squares(step)
                 if step >= LAG:
                     p = step - LAG
                     real, imag = load_f(p)
-                    finish(p, (eye_both + real, imag), (work[p, 0], work[p, 1]))
+                    if p >= kept:
+                        keep(p, [eye_both + real, imag, work[p, 0], work[p, 1]])
+                    else:
+                        finish(flat, p, (eye_both + real, imag), (work[p, 0], work[p, 1]))
 
         @pl.when(count > 2)
         def _():
+            flat = tools.columns(rows, index)
             for step in range(total_pairs + 2 * LAG):
                 if step < total_pairs:
                     squares(step)
                 if LAG <= step < total_pairs + LAG:
                     cubes(step - LAG)
-                if step >= 2 * LAG:
+                if 2 * LAG <= step < kept + 2 * LAG:
                     p = step - 2 * LAG
-                    finish(p, (work[p, 2], work[p, 3]), (work[p, 4], work[p, 5]))
+                    finish(flat, p, (work[p, 2], work[p, 3]), (work[p, 4], work[p, 5]))
 
         return carry
 
@@ -609,17 +641,19 @@
 
 def newton(f_values, rows, counts):
     column, slots, pairs, _, orbitals, width = f_values.shape
-    depth = 2 * slots * pairs * width
+    depth = 2 * (slots * pairs - TAIL) * width
     return pl.pallas_call(
         newton_kernel,
         out_shape=(
             jax.ShapeDtypeStruct((column, 2 * orbitals, depth), jnp.bfloat16),
             jax.ShapeDtypeStruct((column, depth, 2 * width), jnp.bfloat16),
+            jax.ShapeDtypeStruct((column, TAIL, 4, orbitals, width), jnp.float32),
         ),
         in_specs=[VMEM] * 3,
-        out_specs=(VMEM, VMEM),
+        out_specs=(VMEM,) * 3,
         scratch_shapes=[
             pltpu.VMEM((slots * pairs, 6, orbitals, width), jnp.float32),
+            pltpu.VMEM((slots * pairs, 2, orbitals, 2 * width), jnp.bfloat16),
             pltpu.SMEM((column,), jnp.int32),
         ],
         compiler_params=pltpu.CompilerParams(vmem_limit_bytes=GRANT),
@@ -627,7 +661,23 @@
     )(f_values, rows, counts)
 
 
-def scatter_kernel(left_ref, right_ref, sg_ref, weights_hbm, out_ref, weights, part, landed, load_sem, send, recv):
+def scatter_kernel(
+    left_ref,
+    right_ref,
+    tail_ref,
+    rows,
+    sg_ref,
+    weights_hbm,
+    out_ref,
+    weights,
+    left_tail,
+    right_tail,
+    part,
+    landed,
+    load_sem,
+    send,
+    recv,
+):
     freq_devs = lax.axis_size("freq")
     group_devs = lax.axis_size("kgrp")
     column, _, orbitals, width = sg_ref.shape
@@ -657,16 +707,27 @@
         )
 
     wide_left = lax.broadcasted_iota(jnp.int32, (orbitals, width), 1) < orbitals
-    depth = left_ref.shape[2]
+    tools = Tools(orbitals, width)
+    pairs = rows.shape[2] // 2
+    tail = tail_ref.shape[1]
+    kept = rows.shape[1] * pairs - tail
+    for index in range(column):
+        flat = tools.columns(rows, index)
+        for at in range(tail):
+            high, low = parts(*tools.scaled(flat, pairs, kept + at, tail_ref[index, at, 0], tail_ref[index, at, 1]))
+            tools.store_left(left_tail, index, at, high, low)
+            tools.store_right(right_tail, index, at, tail_ref[index, at, 2], tail_ref[index, at, 3])
     step = 2 * width
+    chunks = [(left_ref, right_ref, at * step) for at in range(kept)]
+    chunks += [(left_tail, right_tail, at * step) for at in range(tail)]
     products = []
     for first in range(0, column, 2):
         sums = [None, None]
-        for at in range(0, depth, step):
+        for left_side, right_side, at in chunks:
             for offset in range(2):
                 index = first + offset
-                term = dot(left_ref[index, :, at : at + step], right_ref[index, at : at + step, :])
-                sums[offset] = term if at == 0 else sums[offset] + term
+                term = dot(left_side[index, :, at : at + step], right_side[index, at : at + step, :])
+                sums[offset] = term if sums[offset] is None else sums[offset] + term
         products += sums
     for index in range(column):
         guess = sg_ref[index, 1]
@@ -709,17 +770,19 @@
         spread(index).wait_send()
 
 
-def scatter(left, right, sigma_guess, weights, freq_devs, group_devs):
+def scatter(left, right, rest, rows, sigma_guess, weights, freq_devs, group_devs):
     column, _, orbitals, width = sigma_guess.shape
     tile = column * orbitals // (freq_devs * group_devs)
     peers = freq_devs * group_devs - 1
     return pl.pallas_call(
         scatter_kernel,
         out_shape=jax.ShapeDtypeStruct((8 * column, width), jnp.float32),
-        in_specs=[VMEM, VMEM, VMEM, HBM],
+        in_specs=[VMEM] * 5 + [HBM],
         out_specs=VMEM,
         scratch_shapes=[
             pltpu.VMEM(weights.shape, jnp.int32),
+            pltpu.VMEM((column, 2 * orbitals, 2 * TAIL * width), jnp.bfloat16),
+            pltpu.VMEM((column, 2 * TAIL * width, 2 * width), jnp.bfloat16),
             pltpu.VMEM((column * orbitals, width), jnp.float32),
             pltpu.VMEM((freq_devs, group_devs, tile, width), jnp.float32),
             pltpu.SemaphoreType.DMA((1,)),
@@ -728,7 +791,7 @@
         ],
         compiler_params=pltpu.CompilerParams(collective_id=1, has_side_effects=True, vmem_limit_bytes=GRANT),
         name="scatter",
-    )(left, right, sigma_guess, weights)
+    )(left, right, rest, rows, sigma_guess, weights)
 
 
 def per_device(hamiltonian, self_energy, guess_factor, weights, counts):
@@ -756,8 +819,8 @@
             for value in (hamiltonian, self_energy, guess_factor, table, counts.reshape(1, -1))
         ]
         values, rows, sigma_guess, steps = gather(*inputs, column)
-        left, right = newton(values, rows, steps)
-        return scatter(left, right, sigma_guess, inputs[3], freq_devs, group_devs).T
+        left, right, rest = newton(values, rows, steps)
+        return scatter(left, right, rest, rows, sigma_guess, inputs[3], freq_devs, group_devs).T
     sigma = lax.all_gather(self_energy, "freq", axis=0, tiled=True)
     guess = lax.all_gather(guess_factor, "freq", axis=0, tiled=True)
     current, factors = early_steps(counts, weights, hamiltonian, sigma, guess)

time: 27.2 us -> 25.8 us (0.949)
  Pallas kernels: 26.6 us -> 25 us
    pallas_call x1, Pallas kernels: 5.79 us -> 3.07 us  [newton(): pl.pallas_call(newton_kernel, out_shape=(jax.ShapeDtypeStruct((column, 2...]
    pallas_call x1, Pallas kernels: 8.62 us -> 9.54 us  [scatter(): pl.pallas_call(scatter_kernel, out_shape=jax.ShapeDtypeStruct((8 * column...]
where the time goes in v1:
time: 25.8 us; the launch traced here: 25.6 us
  Pallas kernels  25 us (97%)
  local copies, waits for them, and re-layouts  0.61 us (2%)
    pallas_call x1, Pallas kernels, gather(): pl.pallas_call(gather_kernel, out_shape=(jax.ShapeDtypeStruct((column, 4,...  12.4 us
    pallas_call x1, Pallas kernels, scatter(): pl.pallas_call(scatter_kernel, out_shape=jax.ShapeDtypeStruct((8 * column...  9.54 us
    pallas_call x1, Pallas kernels, newton(): pl.pallas_call(newton_kernel, out_shape=(jax.ShapeDtypeStruct((column, 2...  3.07 us
    unnamed x1, local copies, waits for them, and re-layouts  0.61 us

profile of v1, /device:TPU:0, one launch (start us, length us, event | category | flops | bytes accessed | tf_op | source)
XLA Modules:
  0.0 25.6 jit_solution(7514043272726305572)
XLA Ops:
  0.0 12.4 %gather.1 = (f32[4,4,4,2,64,128]{5,4,3,2,1,0:T(8,128)S(1)}, f32[4,4,8,128]{3,2,1,0:T(8,128)S(1)}, f32[4,2,64,128]{3,2,1,0:T(8,128)S(1)}, s32[1,16]{1,0:T(1,128)S(1)}) custom-call(f32[8,64,128]{2,1,0:T(8,128)} %h_hbm.1, f32[2,64,128]{2,1,0:T(8,128)} %sigma_hbm.1, f32[2,64,128]{2,1,0:T(8,128)} %guess_hbm.1, s32[2,128]{1,0:T(2,128)} %bitcast.4, s32[1,16]{1,0:T(1,128)} %bitcast.6), custom_call_target="tpu_custom_call" | custom-call | tf_op jit(solution)/shard_map/gather/pallas_call | solution.py:426
  12.4 3.1 %newton.1 = (bf16[4,128,3072]{2,1,0:T(8,128)(2,1)S(1)}, bf16[4,3072,256]{2,1,0:T(8,128)(2,1)S(1)}, f32[4,4,4,64,128]{4,3,2,1,0:T(8,128)S(1)}) custom-call(f32[4,4,4,2,64,128]{5,4,3,2,1,0:T(8,128)S(1)} %get-tuple-element.12.f_ref, f32[4,4,8,128]{3,2,1,0:T(8,128)S(1)} %get-tuple-element.13.rows, s32[1,16]{1,0:T(1,128)S(1)} %get-tuple-element.14.counts_ref), custom_call_target="tpu_custom_call" | custom-call | tf_op jit(solution)/shard_map/newton/pallas_call | solution.py:645
  15.5 9.5 %scatter.1 = f32[32,128]{1,0:T(8,128)S(1)} custom-call(bf16[4,128,3072]{2,1,0:T(8,128)(2,1)S(1)} %get-tuple-element.15.left_ref, bf16[4,3072,256]{2,1,0:T(8,128)(2,1)S(1)} %get-tuple-element.16.right_ref, f32[4,4,4,64,128]{4,3,2,1,0:T(8,128)S(1)} %get-tuple-element.17.tail_ref, f32[4,4,8,128]{3,2,1,0:T(8,128)S(1)} %get-tuple-element.13.rows, ...), custom_call_target="tpu_custom_call" | custom-call | tf_op jit(solution)/shard_map/scatter/pallas_call | solution.py:777
  25.0 0.6 %copy.7 = f32[128,32]{0,1:T(8,128)} copy(f32[128,32]{0,1:T(8,128)S(1)} %bitcast.3) | data formatting | bytes 32768

commit v2 on v1

--- a/solution.py
+++ b/solution.py
@@ -320,7 +320,7 @@
     loads[1].wait()
     loads[2].wait()
     pl.semaphore_wait(barrier, column + 1)
-    for copy in across + columns + [beside]:
+    for copy in columns + across + [beside]:
         copy.start()
     loads[3].wait()
     loads[4].wait()
@@ -690,8 +690,9 @@
     def place(step):
         return lax.rem(me + step[0], freq_devs), lax.rem(group + step[1], group_devs)
 
-    for step in others:
-        pl.semaphore_signal(barrier, inc=1, device_id=place(step), device_id_type=MESH)
+    for freq_to in range(freq_devs):
+        for group_to in range(group_devs):
+            pl.semaphore_signal(barrier, inc=1, device_id=(freq_to, group_to), device_id_type=MESH)
     load = pltpu.make_async_copy(weights_hbm, weights, load_sem.at[0])
     load.start()
 
@@ -739,9 +740,27 @@
         left_side = jnp.concatenate(halves(total), 1)
         green = joined(dot(left_side, jnp.concatenate([top, bottom, top, bottom], 0)))
         part[pl.ds(index, orbitals, stride=column), :] = green
-    pl.semaphore_wait(barrier, len(others))
-    for index in range(len(others)):
-        spread(index).start()
+    pl.semaphore_wait(barrier, len(others) + 1)
+
+    def send_to(freq_to, group_to):
+        ahead = lax.rem(freq_to - me + freq_devs, freq_devs)
+        aside = lax.rem(group_to - group + group_devs, group_devs)
+        slot = ahead * group_devs + aside - 1
+        pltpu.make_async_remote_copy(
+            src_ref=part.at[pl.ds((freq_to * group_devs + group_to) * tile, tile)],
+            dst_ref=landed.at[me, group],
+            send_sem=send.at[slot],
+            recv_sem=recv.at[slot],
+            device_id=(freq_to, group_to),
+            device_id_type=MESH,
+        ).start()
+
+    for at in range(freq_devs - 1):
+        freq_to = at + (at >= me).astype(jnp.int32)
+        for group_to in range(group_devs):
+            send_to(freq_to, jnp.int32(group_to))
+    for at in range(group_devs - 1):
+        send_to(me, at + (at >= group).astype(jnp.int32))
     landed[me, group] = part[pl.ds((me * group_devs + group) * tile, tile), :]
     load.wait()
     total = jnp.sum(weights[...].astype(jnp.float32), axis=0, keepdims=True)

time: 25.8 us -> 25 us (0.969)
  Pallas kernels: 25 us -> 23.9 us
    pallas_call x1, Pallas kernels: 9.54 us -> 8.49 us  [scatter(): pl.pallas_call(scatter_kernel, out_shape=jax.ShapeDtypeStruct((8 * column...]
where the time goes in v2:
time: 25 us; the launch traced here: 24.6 us
  Pallas kernels  23.9 us (96%)
  local copies, waits for them, and re-layouts  0.61 us (2%)
    pallas_call x1, Pallas kernels, gather(): pl.pallas_call(gather_kernel, out_shape=(jax.ShapeDtypeStruct((column, 4,...  12.4 us
    pallas_call x1, Pallas kernels, scatter(): pl.pallas_call(scatter_kernel, out_shape=jax.ShapeDtypeStruct((8 * column...  8.49 us
    pallas_call x1, Pallas kernels, newton(): pl.pallas_call(newton_kernel, out_shape=(jax.ShapeDtypeStruct((column, 2...  3.07 us
    unnamed x1, local copies, waits for them, and re-layouts  0.61 us

profile of v2, /device:TPU:0, one launch (start us, length us, event | category | flops | bytes accessed | tf_op | source)
XLA Modules:
  0.0 24.6 jit_solution(14617955946746234922)
XLA Ops:
  0.0 12.4 %gather.1 = (f32[4,4,4,2,64,128]{5,4,3,2,1,0:T(8,128)S(1)}, f32[4,4,8,128]{3,2,1,0:T(8,128)S(1)}, f32[4,2,64,128]{3,2,1,0:T(8,128)S(1)}, s32[1,16]{1,0:T(1,128)S(1)}) custom-call(f32[8,64,128]{2,1,0:T(8,128)} %h_hbm.1, f32[2,64,128]{2,1,0:T(8,128)} %sigma_hbm.1, f32[2,64,128]{2,1,0:T(8,128)} %guess_hbm.1, s32[2,128]{1,0:T(2,128)} %bitcast.4, s32[1,16]{1,0:T(1,128)} %bitcast.6), custom_call_target="tpu_custom_call" | custom-call | tf_op jit(solution)/shard_map/gather/pallas_call | solution.py:426
  12.4 3.1 %newton.1 = (bf16[4,128,3072]{2,1,0:T(8,128)(2,1)S(1)}, bf16[4,3072,256]{2,1,0:T(8,128)(2,1)S(1)}, f32[4,4,4,64,128]{4,3,2,1,0:T(8,128)S(1)}) custom-call(f32[4,4,4,2,64,128]{5,4,3,2,1,0:T(8,128)S(1)} %get-tuple-element.12.f_ref, f32[4,4,8,128]{3,2,1,0:T(8,128)S(1)} %get-tuple-element.13.rows, s32[1,16]{1,0:T(1,128)S(1)} %get-tuple-element.14.counts_ref), custom_call_target="tpu_custom_call" | custom-call | tf_op jit(solution)/shard_map/newton/pallas_call | solution.py:645
  15.5 8.5 %scatter.1 = f32[32,128]{1,0:T(8,128)S(1)} custom-call(bf16[4,128,3072]{2,1,0:T(8,128)(2,1)S(1)} %get-tuple-element.15.left_ref, bf16[4,3072,256]{2,1,0:T(8,128)(2,1)S(1)} %get-tuple-element.16.right_ref, f32[4,4,4,64,128]{4,3,2,1,0:T(8,128)S(1)} %get-tuple-element.17.tail_ref, f32[4,4,8,128]{3,2,1,0:T(8,128)S(1)} %get-tuple-element.13.rows, ...), custom_call_target="tpu_custom_call" | custom-call | tf_op jit(solution)/shard_map/scatter/pallas_call | solution.py:796
  24.0 0.6 %copy.7 = f32[128,32]{0,1:T(8,128)} copy(f32[128,32]{0,1:T(8,128)S(1)} %bitcast.3) | data formatting | bytes 32768

commit v3 on v2

--- a/solution.py
+++ b/solution.py
@@ -721,15 +721,18 @@
     step = 2 * width
     chunks = [(left_ref, right_ref, at * step) for at in range(kept)]
     chunks += [(left_tail, right_tail, at * step) for at in range(tail)]
-    products = []
-    for first in range(0, column, 2):
-        sums = [None, None]
-        for left_side, right_side, at in chunks:
-            for offset in range(2):
-                index = first + offset
+    products = [None] * column
+
+    def add(first, some):
+        for left_side, right_side, at in some:
+            for index in range(column):
                 term = dot(left_side[index, :, at : at + step], right_side[index, at : at + step, :])
-                sums[offset] = term if sums[offset] is None else sums[offset] + term
-        products += sums
+                products[index] = term if products[index] is None else products[index] + term
+
+    for first in range(0, column, column):
+        add(first, chunks[:kept])
+    for first in range(0, column, column):
+        add(first, chunks[kept:])
     for index in range(column):
         guess = sg_ref[index, 1]
         turned = pltpu.roll(guess, orbitals, 1)

time: 25 us -> 25.4 us (1.016)
  Pallas kernels: 23.9 us -> 24.6 us
    pallas_call x1, Pallas kernels: 3.07 us -> 3.81 us  [newton(): pl.pallas_call(newton_kernel, out_shape=(jax.ShapeDtypeStruct((column, 2...]
where the time goes in v3:
time: 25.4 us; the launch traced here: 25.2 us
  Pallas kernels  24.6 us (97%)
  local copies, waits for them, and re-layouts  0.61 us (2%)
    pallas_call x1, Pallas kernels, gather(): pl.pallas_call(gather_kernel, out_shape=(jax.ShapeDtypeStruct((column, 4,...  12.4 us
    pallas_call x1, Pallas kernels, scatter(): pl.pallas_call(scatter_kernel, out_shape=jax.ShapeDtypeStruct((8 * column...  8.4 us
    pallas_call x1, Pallas kernels, newton(): pl.pallas_call(newton_kernel, out_shape=(jax.ShapeDtypeStruct((column, 2...  3.81 us
    unnamed x1, local copies, waits for them, and re-layouts  0.61 us

profile of v3, /device:TPU:0, one launch (start us, length us, event | category | flops | bytes accessed | tf_op | source)
XLA Modules:
  0.0 25.2 jit_solution(8716421421687476770)
XLA Ops:
  0.0 12.4 %gather.1 = (f32[4,4,4,2,64,128]{5,4,3,2,1,0:T(8,128)S(1)}, f32[4,4,8,128]{3,2,1,0:T(8,128)S(1)}, f32[4,2,64,128]{3,2,1,0:T(8,128)S(1)}, s32[1,16]{1,0:T(1,128)S(1)}) custom-call(f32[8,64,128]{2,1,0:T(8,128)} %h_hbm.1, f32[2,64,128]{2,1,0:T(8,128)} %sigma_hbm.1, f32[2,64,128]{2,1,0:T(8,128)} %guess_hbm.1, s32[2,128]{1,0:T(2,128)} %bitcast.4, s32[1,16]{1,0:T(1,128)} %bitcast.6), custom_call_target="tpu_custom_call" | custom-call | tf_op jit(solution)/shard_map/gather/pallas_call | solution.py:426
  12.4 3.8 %newton.1 = (bf16[4,128,3072]{2,1,0:T(8,128)(2,1)S(1)}, bf16[4,3072,256]{2,1,0:T(8,128)(2,1)S(1)}, f32[4,4,4,64,128]{4,3,2,1,0:T(8,128)S(1)}) custom-call(f32[4,4,4,2,64,128]{5,4,3,2,1,0:T(8,128)S(1)} %get-tuple-element.12.f_ref, f32[4,4,8,128]{3,2,1,0:T(8,128)S(1)} %get-tuple-element.13.rows, s32[1,16]{1,0:T(1,128)S(1)} %get-tuple-element.14.counts_ref), custom_call_target="tpu_custom_call" | custom-call | tf_op jit(solution)/shard_map/newton/pallas_call | solution.py:645
  16.2 8.4 %scatter.1 = f32[32,128]{1,0:T(8,128)S(1)} custom-call(bf16[4,128,3072]{2,1,0:T(8,128)(2,1)S(1)} %get-tuple-element.15.left_ref, bf16[4,3072,256]{2,1,0:T(8,128)(2,1)S(1)} %get-tuple-element.16.right_ref, f32[4,4,4,64,128]{4,3,2,1,0:T(8,128)S(1)} %get-tuple-element.17.tail_ref, f32[4,4,8,128]{3,2,1,0:T(8,128)S(1)} %get-tuple-element.13.rows, ...), custom_call_target="tpu_custom_call" | custom-call | tf_op jit(solution)/shard_map/scatter/pallas_call | solution.py:799
  24.6 0.6 %copy.7 = f32[128,32]{0,1:T(8,128)} copy(f32[128,32]{0,1:T(8,128)S(1)} %bitcast.3) | data formatting | bytes 32768
